TPU v7x, 512 devices: a 4x2x32 block of a 4x16x32 slice. The times are simulated.
512 devices in a mesh: member: 2 (over y), lat: 32 (over z), lon: 4 (over x), lev: 2 (over core).
Axes of the slice: x: 4, y: 2, z: 32, core: 2. Of those that a mesh axis runs over, the one named last changes fastest.
The devices are a block of a 4x16x32 slice.
Arguments:
- perturbation: bfloat16 [4, 64, 128, 16, 128], P('member', 'lev', 'lat', 'lon'), parts along dimension 0, may hold values from -6 to 6
- adjoint_forcing: bfloat16 [4, 64, 128, 16, 128], P('member', 'lev', 'lat', 'lon'), parts along dimension 0, may hold values from -6 to 6
- source_rows: int32 [128, 16, 4], P('lat', 'lon'), may hold values from 0 to 127, as said below
- source_cols: int32 [128, 16, 4], P('lat', 'lon'), may hold values from 0 to 15, as said below
- cubic_weights: bfloat16 [128, 16, 4, 128, 128], P('lat', 'lon'), may hold values from -1.5 to 1.5
Outputs:
- tangent_out: bfloat16 [4, 64, 128, 16, 128], P('member', 'lev', 'lat', 'lon'), parts along dimension 0
- adjoint_out: bfloat16 [4, 64, 128, 16, 128], P('member', 'lev', 'lat', 'lon'), parts along dimension 0
There are 2 independent parts, one for each index of `member`. A program takes and returns all parts, laid end to end along the dimension named above; an argument that names none is the same for every part. Nothing has to cross between parts.
Inputs may be any that keep to these rules, and one draw needn't show every extreme that they name: source_rows[i, j, k] differs from i by at most 8. source_cols[i, j, k] is j + d modulo 16 with d from -1 to 1, and from -2 to 2 where i lies in the first or last 4 block rows.
All inputs are finite; a program needn't handle non-finite values.
Results may differ from a plain program's by a relative error of at most 0.004.
Values may be sent and summed in bfloat16 or wider, within the bound.
No kernel may reach another device: no remote copies, remote signals or barrier semaphores. Data moves between devices by JAX's collectives and lax.ppermute only.
A program may use at most 64 MiB of HBM per device.

v0:
```python
import jax
import jax.numpy as jnp
from jax import lax
from jax.sharding import PartitionSpec as P


def passed_along(array, axis, by):
    devices = lax.axis_size(axis)
    pairs = [(i, i + by) for i in range(devices) if 0 <= i + by < devices]
    return lax.ppermute(array, axis, pairs)


def padded(cells, sides, width):
    for axis, dim in sides:
        count = lax.axis_size(axis)
        head = lax.slice_in_dim(cells, 0, width, axis=dim)
        tail = lax.slice_in_dim(cells, cells.shape[dim] - width, cells.shape[dim], axis=dim)
        cells = jnp.concatenate(
            [
                lax.ppermute(tail, axis, [(i, (i + 1) % count) for i in range(count)]),
                cells,
                lax.ppermute(head, axis, [((i + 1) % count, i) for i in range(count)]),
            ],
            axis=dim,
        )
    return cells


def shifted(array, axis, by):
    devices = lax.axis_size(axis)
    return lax.ppermute(array, axis, [(i, (i + by) % devices) for i in range(devices)])


def rows_extend(tile_data):
    return jnp.concatenate(
        [
            passed_along(tile_data, "lat", 2),
            passed_along(tile_data, "lat", 1),
            tile_data,
            passed_along(tile_data, "lat", -1),
            passed_along(tile_data, "lat", -2),
        ],
        axis=2,
    )


def cols_extend(tile_data):
    return padded(tile_data, (("lon", 3),), 2)


def on_device(perturbation, adjoint_forcing, source_rows, source_cols, cubic_weights):
    fields, levels, band_rows, tile_cols, cell_count = perturbation.shape
    stencil = source_rows.shape[2]
    reach_rows = 2 * band_rows
    row_count = fields * levels
    span_cols = tile_cols + 4
    height = band_rows + 2 * reach_rows
    places = height * span_cols
    targets = band_rows * tile_cols
    extended = cols_extend(rows_extend(perturbation))
    flattened = extended.reshape(row_count, places, cell_count)
    band_index = lax.axis_index("lat")
    tile_index = lax.axis_index("lon")
    total_cols = tile_cols * lax.axis_size("lon")
    local_rows = source_rows - band_index * band_rows + reach_rows
    local_cols = jnp.mod(source_cols - tile_index * tile_cols + 2, total_cols)
    positions = (local_rows * span_cols + local_cols).reshape(-1)
    gathered = jnp.take(flattened, positions, axis=1).reshape(
        row_count, targets, stencil, cell_count
    )
    weights = cubic_weights.reshape(targets, stencil, cell_count, cell_count)
    tangent = jnp.einsum("rtks,tksc->rtc", gathered, weights, preferred_element_type=jnp.float32)
    tangent_out = tangent.astype(jnp.bfloat16).reshape(
        fields, levels, band_rows, tile_cols, cell_count
    )
    forcing = adjoint_forcing.reshape(row_count, targets, cell_count)
    contributions = jnp.einsum(
        "rtc,tksc->rtks", forcing, weights, preferred_element_type=jnp.float32
    )
    contributions = contributions.reshape(row_count, targets * stencil, cell_count)
    onehot = (positions[:, None] == jnp.arange(places, dtype=jnp.int32)[None, :]).astype(
        jnp.float32
    )
    spread = jnp.einsum("rms,mn->rns", contributions, onehot, precision=lax.Precision.HIGHEST)
    spread = spread.reshape(row_count, height, span_cols, cell_count)
    from_east = shifted(spread[:, :, 0:2].astype(jnp.bfloat16), "lon", -1).astype(jnp.float32)
    from_west = shifted(spread[:, :, span_cols - 2 : span_cols], "lon", 1)
    inner_part = spread[:, :, 2 : tile_cols + 2]
    inner_part = inner_part.at[:, :, tile_cols - 2 : tile_cols].add(from_east)
    inner_part = inner_part.at[:, :, 0:2].add(from_west)
    lower_far_part = inner_part[:, 0:band_rows]
    lower_near_part = inner_part[:, band_rows : 2 * band_rows]
    owned = inner_part[:, 2 * band_rows : 3 * band_rows]
    upper_near_part = inner_part[:, 3 * band_rows : 4 * band_rows]
    upper_far_part = inner_part[:, 4 * band_rows : 5 * band_rows]
    owned = owned + passed_along(lower_near_part, "lat", -1)
    owned = owned + passed_along(lower_far_part, "lat", -2)
    owned = owned + passed_along(upper_near_part, "lat", 1)
    owned = owned + passed_along(upper_far_part, "lat", 2)
    adjoint_out = owned.astype(jnp.bfloat16).reshape(
        fields, levels, band_rows, tile_cols, cell_count
    )
    return (tangent_out, adjoint_out)


def solution(mesh):
    placed = (
        P("member", "lev", "lat", "lon", None),
        P("member", "lev", "lat", "lon", None),
        P("lat", "lon", None),
        P("lat", "lon", None),
        P("lat", "lon", None, None, None),
    )
    return jax.shard_map(
        on_device,
        mesh=mesh,
        in_specs=placed,
        out_specs=(P("member", "lev", "lat", "lon", None), P("member", "lev", "lat", "lon", None)),
        check_vma=False,
    )
```

profile of v0, /device:TPU:288, one launch (start us, length us, event | category | flops | bytes accessed | tf_op | source)
XLA Modules:
  0.0 132.9 jit_solution(4381596180967302278)
XLA Ops:
  2.3 1.8 %fusion.11 = f32[16,4,128,64]{2,3,1,0:T(8,128)S(1)} fusion(bf16[16,4,128,128]{3,2,1,0:T(8,128)(2,1)S(1)} %bitcast.33, bf16[64,16,128,1]{2,1,0,3:T(8,128)(2,1)} %bitcast.37), kind=kOutput, calls=%fused_computation.19 | convolution fusion | flops 134217728 | bytes 4456448 | tf_op jit(solution)/shard_map/rtc,tksc->rtks/dot_general | solution.py:77
  4.1 3.5 %convolution_bitcast_fusion = f32[64,20,8,128]{3,2,1,0:T(8,128)S(1)} fusion(f32[64,64,128]{2,0,1:T(8,128)S(1)} %bitcast.34, s32[64]{0:T(128)S(1)} %reshape.146), kind=kOutput, calls=%fused_computation.2 | convolution fusion | flops 1006643200 | bytes 7340288 | tf_op jit(solution)/shard_map/rms,mn->rns/dot_general | solution.py:84
  8.0 5.1 %collective-permute-start.6 = (bf16[64,20,2,128]{3,2,1,0:T(2,128)(2,1)S(1)}, bf16[64,20,2,128]{3,2,1,0:T(2,128)(2,1)S(1)}, u32[]{:S(2)}, u32[]{:S(2)}) collective-permute-start(bf16[64,20,2,128]{3,2,1,0:T(2,128)(2,1)S(1)} %slice.132), channel_id=1, source_target_pairs={{0,6},{2,0},{4,2},{6,4},{1,7},{3,1},{5,3},{7,5},{8,14},{10,8},{12,... | collective-permute-start | bytes 1966088 | tf_op jit(solution)/shard_map/ppermute | solution.py:31
  13.9 8.1 %collective-permute-start = (bf16[2,32,4,4,128]{4,1,3,2,0:T(8,128)(2,1)}, bf16[2,32,4,4,128]{4,1,3,2,0:T(8,128)(2,1)}, u32[]{:S(2)}, u32[]{:S(2)}) collective-permute-start(bf16[2,32,4,4,128]{4,1,3,2,0:T(8,128)(2,1)} %copy.21), channel_id=1, source_target_pairs={{0,16},{8,24},{16,32},{24,40},{32,48},{40,56},{48,64},{56,72},{64,... | collective-permute-start | bytes 786440 | tf_op jit(solution)/shard_map/ppermute | solution.py:10
  22.0 4.7 %collective-permute-start.1 = (bf16[2,32,4,4,128]{4,1,3,2,0:T(8,128)(2,1)}, bf16[2,32,4,4,128]{4,1,3,2,0:T(8,128)(2,1)}, u32[]{:S(2)}, u32[]{:S(2)}) collective-permute-start(bf16[2,32,4,4,128]{4,1,3,2,0:T(8,128)(2,1)} %copy.21), channel_id=1, source_target_pairs={{0,8},{8,16},{16,24},{24,32},{32,40},{40,48},{48,56},{56,64},{64,7... | collective-permute-start | bytes 786440 | tf_op jit(solution)/shard_map/ppermute | solution.py:10
  26.8 2.0 %collective-permute-start.2 = (bf16[2,32,4,4,128]{4,1,3,2,0:T(8,128)(2,1)}, bf16[2,32,4,4,128]{4,1,3,2,0:T(8,128)(2,1)}, u32[]{:S(2)}, u32[]{:S(2)}) collective-permute-start(bf16[2,32,4,4,128]{4,1,3,2,0:T(8,128)(2,1)} %copy.21), channel_id=1, source_target_pairs={{8,0},{16,8},{24,16},{32,24},{40,32},{48,40},{56,48},{64,56},{72,6... | collective-permute-start | bytes 786440 | tf_op jit(solution)/shard_map/ppermute | solution.py:10
  28.7 27.2 %collective-permute-start.3 = (bf16[2,32,4,4,128]{4,1,3,2,0:T(8,128)(2,1)}, bf16[2,32,4,4,128]{4,1,3,2,0:T(8,128)(2,1)}, u32[]{:S(2)}, u32[]{:S(2)}) collective-permute-start(bf16[2,32,4,4,128]{4,1,3,2,0:T(8,128)(2,1)} %copy.21), channel_id=1, source_target_pairs={{16,0},{24,8},{32,16},{40,24},{48,32},{56,40},{64,48},{72,56},{80,... | collective-permute-start | bytes 786440 | tf_op jit(solution)/shard_map/ppermute | solution.py:10
  55.9 2.1 %slice.106 = f32[64,20,4,128]{3,2,1,0:T(4,128)} slice(f32[64,20,8,128]{3,2,1,0:T(8,128)S(1)} %convolution_bitcast_fusion), slice={[0:64], [0:20], [2:6], [0:128]} | slice | bytes 5242880 | tf_op jit(solution)/shard_map/slice | solution.py:88
  58.1 7.0 %fusion.20 = (f32[64,20,2,128]{3,2,1,0:T(2,128)}, f32[64,20,4,128]{3,2,1,0:T(4,128)}) fusion(f32[64,20,8,128]{3,2,1,0:T(8,128)} %copy-done.1, f32[64,20,4,128]{3,2,1,0:T(4,128)} %slice.106, bf16[64,20,2,128]{3,2,1,0:T(2,128)(2,1)S(1)} %collective-permute-done.6), kind=kLoop, calls=%fused_computation.40 | loop fusion | flops 655360 | bytes 5898240 | tf_op jit(solution)/shard_map/slice | solution.py:87
  65.1 3.9 %collective-permute-start.7 = (f32[64,20,2,128]{3,2,1,0:T(2,128)}, f32[64,20,2,128]{3,2,1,0:T(2,128)}, u32[]{:S(2)}, u32[]{:S(2)}) collective-permute-start(f32[64,20,2,128]{3,2,1,0:T(2,128)} %get-tuple-element.32), channel_id=1, source_target_pairs={{0,2},{2,4},{4,6},{6,0},{1,3},{3,5},{5,7},{7,1},{8,10},{10,12},{12... | collective-permute-start | bytes 3932168 | tf_op jit(solution)/shard_map/ppermute | solution.py:31
  75.5 1.9 %collective-permute-start.4 = (bf16[2,32,20,2,128]{4,1,3,2,0:T(8,128)(2,1)S(1)}, bf16[2,32,20,2,128]{4,1,3,2,0:T(8,128)(2,1)}, u32[]{:S(2)}, u32[]{:S(2)}) collective-permute-start(bf16[2,32,20,2,128]{4,1,3,2,0:T(8,128)(2,1)S(1)} %get-tuple-element.38), channel_id=1, source_target_pairs={{0,2},{2,4},{4,6},{6,0},{1,3},{3,5},{5,7},{7,1},{8,10},{10,12},{12... | collective-permute-start | bytes 1966088 | tf_op jit(solution)/shard_map/ppermute | solution.py:20
  77.5 5.2 %collective-permute-start.5 = (bf16[2,32,20,2,128]{4,1,3,2,0:T(8,128)(2,1)}, bf16[2,32,20,2,128]{4,1,3,2,0:T(8,128)(2,1)}, u32[]{:S(2)}, u32[]{:S(2)}) collective-permute-start(bf16[2,32,20,2,128]{4,1,3,2,0:T(8,128)(2,1)} %get-tuple-element.39), channel_id=1, source_target_pairs={{2,0},{4,2},{6,4},{0,6},{3,1},{5,3},{7,5},{1,7},{10,8},{12,10},{14... | collective-permute-start | bytes 1966088 | tf_op jit(solution)/shard_map/ppermute | solution.py:22
  82.7 3.5 %collective-permute-done.7 = f32[64,20,2,128]{3,2,1,0:T(2,128)} collective-permute-done((f32[64,20,2,128]{3,2,1,0:T(2,128)}, f32[64,20,2,128]{3,2,1,0:T(2,128)}, u32[]{:S(2)}, u32[]{:S(2)}) %collective-permute-start.7) | collective-permute-done | bytes 1310752 | tf_op jit(solution)/shard_map/ppermute | solution.py:31
  86.2 2.4 %fusion.1 = f32[64,20,4,128]{3,2,1,0:T(4,128)S(1)} fusion(f32[64,20,4,128]{3,2,1,0:T(4,128)S(1)} %copy-done.2, f32[64,20,2,128]{3,2,1,0:T(2,128)} %collective-permute-done.7), kind=kLoop, calls=%fused_computation.5 | loop fusion | flops 327680 | bytes 3932160 | tf_op jit(solution)/shard_map/scatter-add | solution.py:90
  88.6 1.8 %fusion.21 = (f32[64,4,4,128]{3,2,1,0:T(4,128)}, f32[64,4,4,128]{3,2,1,0:T(4,128)}, f32[64,4,4,128]{3,2,1,0:T(4,128)}, f32[64,4,4,128]{3,2,1,0:T(4,128)}) fusion(f32[64,20,4,128]{3,2,1,0:T(4,128)S(1)} %fusion.1), kind=kLoop, calls=%fused_computation.41 | loop fusion | bytes 4194304 | tf_op jit(solution)/shard_map/slice | solution.py:92
  90.8 4.6 %collective-permute-start.10 = (f32[64,4,4,128]{3,2,1,0:T(4,128)}, f32[64,4,4,128]{3,2,1,0:T(4,128)}, u32[]{:S(2)}, u32[]{:S(2)}) collective-permute-start(f32[64,4,4,128]{3,2,1,0:T(4,128)} %get-tuple-element.36), channel_id=1, source_target_pairs={{0,8},{8,16},{16,24},{24,32},{32,40},{40,48},{48,56},{56,64},{64,7... | collective-permute-start | bytes 1572872 | tf_op jit(solution)/shard_map/ppermute | solution.py:10
  95.4 2.0 %collective-permute-start.11 = (f32[64,4,4,128]{3,2,1,0:T(4,128)}, f32[64,4,4,128]{3,2,1,0:T(4,128)}, u32[]{:S(2)}, u32[]{:S(2)}) collective-permute-start(f32[64,4,4,128]{3,2,1,0:T(4,128)} %get-tuple-element.35), channel_id=1, source_target_pairs={{0,16},{8,24},{16,32},{24,40},{32,48},{40,56},{48,64},{56,72},{64,... | collective-permute-start | bytes 1572872 | tf_op jit(solution)/shard_map/ppermute | solution.py:10
  97.4 4.2 %collective-permute-start.8 = (f32[64,4,4,128]{3,2,1,0:T(4,128)}, f32[64,4,4,128]{3,2,1,0:T(4,128)}, u32[]{:S(2)}, u32[]{:S(2)}) collective-permute-start(f32[64,4,4,128]{3,2,1,0:T(4,128)} %get-tuple-element.34), channel_id=1, source_target_pairs={{8,0},{16,8},{24,16},{32,24},{40,32},{48,40},{56,48},{64,56},{72,6... | collective-permute-start | bytes 1572872 | tf_op jit(solution)/shard_map/ppermute | solution.py:10
  101.6 3.7 %collective-permute-start.9 = (f32[64,4,4,128]{3,2,1,0:T(4,128)}, f32[64,4,4,128]{3,2,1,0:T(4,128)}, u32[]{:S(2)}, u32[]{:S(2)}) collective-permute-start(f32[64,4,4,128]{3,2,1,0:T(4,128)} %get-tuple-element.37), channel_id=1, source_target_pairs={{16,0},{24,8},{32,16},{40,24},{48,32},{56,40},{64,48},{72,56},{80,... | collective-permute-start | bytes 1572872 | tf_op jit(solution)/shard_map/ppermute | solution.py:10
  107.1 2.2 %copy.26 = bf16[2,32,20,8,128]{4,1,0,3,2:T(8,128)(2,1)} copy(bf16[2,32,20,8,128]{4,1,3,2,0:T(8,128)(2,1)S(1)} %pad_maximum_fusion) | data formatting | bytes 5242880 | tf_op jit(solution)/shard_map/concatenate | solution.py:18
  109.3 2.5 %gather_fusion = bf16[64,64,128]{2,1,0:T(8,128)(2,1)S(1)} fusion(bf16[64,160,128]{2,0,1:T(8,128)(2,1)} %bitcast.35, s32[1024]{0:T(1024)S(1)} %pad_clamp_fusion), kind=kCustom, calls=%fused_computation | custom fusion | bytes 2097408 | tf_op jit(solution)/shard_map/jit(_take)/gather | solution.py:68
  114.5 2.1 %collective-permute-done.8 = f32[64,4,4,128]{3,2,1,0:T(4,128)} collective-permute-done((f32[64,4,4,128]{3,2,1,0:T(4,128)}, f32[64,4,4,128]{3,2,1,0:T(4,128)}, u32[]{:S(2)}, u32[]{:S(2)}) %collective-permute-start.8) | collective-permute-done | bytes 524320 | tf_op jit(solution)/shard_map/ppermute | solution.py:10
  116.6 13.6 %collective-permute-done.9 = f32[64,4,4,128]{3,2,1,0:T(4,128)} collective-permute-done((f32[64,4,4,128]{3,2,1,0:T(4,128)}, f32[64,4,4,128]{3,2,1,0:T(4,128)}, u32[]{:S(2)}, u32[]{:S(2)}) %collective-permute-start.9) | collective-permute-done | bytes 524320 | tf_op jit(solution)/shard_map/ppermute | solution.py:10
  130.2 2.7 %fusion.9 = bf16[64,4,4,128]{3,2,1,0:T(4,128)(2,1)} fusion(f32[64,4,4,128]{3,2,1,0:T(4,128)} %collective-permute-done.11, f32[64,4,4,128]{3,2,1,0:T(4,128)} %collective-permute-done.10, f32[64,4,4,128]{3,2,1,0:T(4,128)} %collective-permute-done.9, f32[64,4,4,128]{3,2,1,0:T(4,128)} %collective-permute-done.8, f32[64,20,4,128]{3,2,1,0:T(4,128)} %copy-done.3), kind=kLoop, calls=%fused_computation.17 | loop fusion | flops 655360 | bytes 2883584 | tf_op jit(solution)/shard_map/convert_element_type | solution.py:100
  (38 shorter events, 14.0 us)
Async XLA Ops:
  0.6 1.6 %copy-start = (bf16[4,4,4,128,128]{4,3,2,1,0:T(8,128)(2,1)S(1)}, bf16[4,4,4,128,128]{4,3,2,1,0:T(8,128)(2,1)}, u32[]{:S(2)}) copy-start(bf16[4,4,4,128,128]{4,3,2,1,0:T(8,128)(2,1)} %param.13) | copy-start | bytes 6291460
  4.0 9.1 %copy-start.4 = (bf16[2,32,4,4,128]{4,3,2,1,0:T(4,128)(2,1)S(1)}, bf16[2,32,4,4,128]{4,3,2,1,0:T(4,128)(2,1)}, u32[]{:S(2)}) copy-start(bf16[2,32,4,4,128]{4,3,2,1,0:T(4,128)(2,1)} %param.9) | copy-start | bytes 786436
  7.6 50.4 %copy-start.1 = (f32[64,20,8,128]{3,2,1,0:T(8,128)}, f32[64,20,8,128]{3,2,1,0:T(8,128)S(1)}, u32[]{:S(2)}) copy-start(f32[64,20,8,128]{3,2,1,0:T(8,128)S(1)} %convolution_bitcast_fusion) | copy-start | bytes 15728644
  8.0 50.1 %collective-permute-start.6 = (bf16[64,20,2,128]{3,2,1,0:T(2,128)(2,1)S(1)}, bf16[64,20,2,128]{3,2,1,0:T(2,128)(2,1)S(1)}, u32[]{:S(2)}, u32[]{:S(2)}) collective-permute-start(bf16[64,20,2,128]{3,2,1,0:T(2,128)(2,1)S(1)} %slice.132), channel_id=1, source_target_pairs={{0,6},{2,0},{4,2},{6,4},{1,7},{3,1},{5,3},{7,5},{8,14},{10,8},{12,... | collective-permute-start | bytes 1966088 | tf_op jit(solution)/shard_map/ppermute | solution.py:31
  13.9 55.3 %collective-permute-start = (bf16[2,32,4,4,128]{4,1,3,2,0:T(8,128)(2,1)}, bf16[2,32,4,4,128]{4,1,3,2,0:T(8,128)(2,1)}, u32[]{:S(2)}, u32[]{:S(2)}) collective-permute-start(bf16[2,32,4,4,128]{4,1,3,2,0:T(8,128)(2,1)} %copy.21), channel_id=1, source_target_pairs={{0,16},{8,24},{16,32},{24,40},{32,48},{40,56},{48,64},{56,72},{64,... | collective-permute-start | bytes 786440 | tf_op jit(solution)/shard_map/ppermute | solution.py:10
  22.0 48.1 %collective-permute-start.1 = (bf16[2,32,4,4,128]{4,1,3,2,0:T(8,128)(2,1)}, bf16[2,32,4,4,128]{4,1,3,2,0:T(8,128)(2,1)}, u32[]{:S(2)}, u32[]{:S(2)}) collective-permute-start(bf16[2,32,4,4,128]{4,1,3,2,0:T(8,128)(2,1)} %copy.21), channel_id=1, source_target_pairs={{0,8},{8,16},{16,24},{24,32},{32,40},{40,48},{48,56},{56,64},{64,7... | collective-permute-start | bytes 786440 | tf_op jit(solution)/shard_map/ppermute | solution.py:10
  26.8 45.6 %collective-permute-start.2 = (bf16[2,32,4,4,128]{4,1,3,2,0:T(8,128)(2,1)}, bf16[2,32,4,4,128]{4,1,3,2,0:T(8,128)(2,1)}, u32[]{:S(2)}, u32[]{:S(2)}) collective-permute-start(bf16[2,32,4,4,128]{4,1,3,2,0:T(8,128)(2,1)} %copy.21), channel_id=1, source_target_pairs={{8,0},{16,8},{24,16},{32,24},{40,32},{48,40},{56,48},{64,56},{72,6... | collective-permute-start | bytes 786440 | tf_op jit(solution)/shard_map/ppermute | solution.py:10
  28.7 44.7 %collective-permute-start.3 = (bf16[2,32,4,4,128]{4,1,3,2,0:T(8,128)(2,1)}, bf16[2,32,4,4,128]{4,1,3,2,0:T(8,128)(2,1)}, u32[]{:S(2)}, u32[]{:S(2)}) collective-permute-start(bf16[2,32,4,4,128]{4,1,3,2,0:T(8,128)(2,1)} %copy.21), channel_id=1, source_target_pairs={{16,0},{24,8},{32,16},{40,24},{48,32},{56,40},{64,48},{72,56},{80,... | collective-permute-start | bytes 786440 | tf_op jit(solution)/shard_map/ppermute | solution.py:10
  65.1 21.0 %collective-permute-start.7 = (f32[64,20,2,128]{3,2,1,0:T(2,128)}, f32[64,20,2,128]{3,2,1,0:T(2,128)}, u32[]{:S(2)}, u32[]{:S(2)}) collective-permute-start(f32[64,20,2,128]{3,2,1,0:T(2,128)} %get-tuple-element.32), channel_id=1, source_target_pairs={{0,2},{2,4},{4,6},{6,0},{1,3},{3,5},{5,7},{7,1},{8,10},{10,12},{12... | collective-permute-start | bytes 3932168 | tf_op jit(solution)/shard_map/ppermute | solution.py:31
  71.2 15.0 %copy-start.2 = (f32[64,20,4,128]{3,2,1,0:T(4,128)S(1)}, f32[64,20,4,128]{3,2,1,0:T(4,128)}, u32[]{:S(2)}) copy-start(f32[64,20,4,128]{3,2,1,0:T(4,128)} %get-tuple-element.33) | copy-start | bytes 7864324
  75.5 26.1 %collective-permute-start.4 = (bf16[2,32,20,2,128]{4,1,3,2,0:T(8,128)(2,1)S(1)}, bf16[2,32,20,2,128]{4,1,3,2,0:T(8,128)(2,1)}, u32[]{:S(2)}, u32[]{:S(2)}) collective-permute-start(bf16[2,32,20,2,128]{4,1,3,2,0:T(8,128)(2,1)S(1)} %get-tuple-element.38), channel_id=1, source_target_pairs={{0,2},{2,4},{4,6},{6,0},{1,3},{3,5},{5,7},{7,1},{8,10},{10,12},{12... | collective-permute-start | bytes 1966088 | tf_op jit(solution)/shard_map/ppermute | solution.py:20
  77.5 28.0 %collective-permute-start.5 = (bf16[2,32,20,2,128]{4,1,3,2,0:T(8,128)(2,1)}, bf16[2,32,20,2,128]{4,1,3,2,0:T(8,128)(2,1)}, u32[]{:S(2)}, u32[]{:S(2)}) collective-permute-start(bf16[2,32,20,2,128]{4,1,3,2,0:T(8,128)(2,1)} %get-tuple-element.39), channel_id=1, source_target_pairs={{2,0},{4,2},{6,4},{0,6},{3,1},{5,3},{7,5},{1,7},{10,8},{12,10},{14... | collective-permute-start | bytes 1966088 | tf_op jit(solution)/shard_map/ppermute | solution.py:22
  88.6 2.2 %copy-start.3 = (f32[64,20,4,128]{3,2,1,0:T(4,128)}, f32[64,20,4,128]{3,2,1,0:T(4,128)S(1)}, u32[]{:S(2)}) copy-start(f32[64,20,4,128]{3,2,1,0:T(4,128)S(1)} %fusion.1) | copy-start | bytes 7864324
  90.8 22.4 %collective-permute-start.10 = (f32[64,4,4,128]{3,2,1,0:T(4,128)}, f32[64,4,4,128]{3,2,1,0:T(4,128)}, u32[]{:S(2)}, u32[]{:S(2)}) collective-permute-start(f32[64,4,4,128]{3,2,1,0:T(4,128)} %get-tuple-element.36), channel_id=1, source_target_pairs={{0,8},{8,16},{16,24},{24,32},{32,40},{40,48},{48,56},{56,64},{64,7... | collective-permute-start | bytes 1572872 | tf_op jit(solution)/shard_map/ppermute | solution.py:10
  95.4 19.1 %collective-permute-start.11 = (f32[64,4,4,128]{3,2,1,0:T(4,128)}, f32[64,4,4,128]{3,2,1,0:T(4,128)}, u32[]{:S(2)}, u32[]{:S(2)}) collective-permute-start(f32[64,4,4,128]{3,2,1,0:T(4,128)} %get-tuple-element.35), channel_id=1, source_target_pairs={{0,16},{8,24},{16,32},{24,40},{32,48},{40,56},{48,64},{56,72},{64,... | collective-permute-start | bytes 1572872 | tf_op jit(solution)/shard_map/ppermute | solution.py:10
  97.4 19.2 %collective-permute-start.8 = (f32[64,4,4,128]{3,2,1,0:T(4,128)}, f32[64,4,4,128]{3,2,1,0:T(4,128)}, u32[]{:S(2)}, u32[]{:S(2)}) collective-permute-start(f32[64,4,4,128]{3,2,1,0:T(4,128)} %get-tuple-element.34), channel_id=1, source_target_pairs={{8,0},{16,8},{24,16},{32,24},{40,32},{48,40},{56,48},{64,56},{72,6... | collective-permute-start | bytes 1572872 | tf_op jit(solution)/shard_map/ppermute | solution.py:10
  101.6 28.6 %collective-permute-start.9 = (f32[64,4,4,128]{3,2,1,0:T(4,128)}, f32[64,4,4,128]{3,2,1,0:T(4,128)}, u32[]{:S(2)}, u32[]{:S(2)}) collective-permute-start(f32[64,4,4,128]{3,2,1,0:T(4,128)} %get-tuple-element.37), channel_id=1, source_target_pairs={{16,0},{24,8},{32,16},{40,24},{48,32},{56,40},{64,48},{72,56},{80,... | collective-permute-start | bytes 1572872 | tf_op jit(solution)/shard_map/ppermute | solution.py:10
where the time goes:
time: 134 us; the launch traced here: 133 us
  starting transfers between devices  72.6 us (54%)
  waiting for transfers between devices  20.5 us (15%)
  local copies, waits for them, and re-layouts  18.3 us (14%)
  other arithmetic  14.7 us (11%)
  matrix products  5.84 us (4%)
    ppermute x8, starting transfers between devices, passed_along(): return lax.ppermute(array, axis, pairs)  56.5 us
    ppermute x8, waiting for transfers between devices, passed_along(): return lax.ppermute(array, axis, pairs)  17 us
    ppermute x2, starting transfers between devices, shifted(): lax.ppermute(array, axis, [(i, (i + by) % devices) for i in range(devices)])  9.05 us
    slice x1, other arithmetic, on_device(): from_west = shifted(spread[:, :, span_cols - 2:span_cols], 'lon', 1)  7.04 us
    unnamed x16, local copies, waits for them, and re-layouts  6.89 us
    ppermute x1, starting transfers between devices, padded(): lax.ppermute(head, axis, [((i + 1) % count, i) for i in range(count)])  5.16 us
    dot_general x1, matrix products, on_device(): jnp.einsum('rms,mn->rns', contributions, onehot, precision=lax.Precision....  3.55 us
    ppermute x2, waiting for transfers between devices, shifted(): lax.ppermute(array, axis, [(i, (i + by) % devices) for i in range(devices)])  3.53 us
  transfers between devices with their start and end apart: 12, of which 4 were waited for; matrix products, arithmetic and copies ran while one was open for 21% of the time, Pallas kernels for 0%

commit v1 on v0

v1 whole, which is shorter than its diff:
```python
import functools

import jax
import jax.numpy as jnp
from jax import lax
from jax.experimental import pallas as pl
from jax.experimental.pallas import tpu as pltpu
from jax.sharding import PartitionSpec as P

VMEM = pl.BlockSpec(memory_space=pltpu.VMEM)
SMEM = pl.BlockSpec(memory_space=pltpu.SMEM)
ANY = pl.BlockSpec(memory_space=pl.ANY)
PARAMS = pltpu.CompilerParams(vmem_limit_bytes=6 << 20)


def passed_along(array, axis, by):
    devices = lax.axis_size(axis)
    pairs = [(i, i + by) for i in range(devices) if 0 <= i + by < devices]
    return lax.ppermute(array, axis, pairs)


def shifted(array, axis, by):
    devices = lax.axis_size(axis)
    return lax.ppermute(array, axis, [(i, (i + by) % devices) for i in range(devices)])


def adjoint_kernel(tile_cols, height, slots, pos_ref, forcing_ref, weights_ref, acc_ref, west_ref, east_ref):
    targets, stencil, cells, _ = weights_ref.shape
    inner = height * tile_cols
    acc_ref[...] = jnp.zeros_like(acc_ref)
    for t in range(targets):
        part = lax.dot_general(
            forcing_ref[t],
            weights_ref[t].reshape(stencil * cells, cells),
            (((1,), (1,)), ((), ())),
            preferred_element_type=jnp.float32,
        )
        for k in range(stencil):
            place = pos_ref[t * stencil + k]
            acc_ref[place] += part[:, k * cells : (k + 1) * cells]
    west_ref[...] = acc_ref[inner : inner + slots].astype(west_ref.dtype)
    east_ref[...] = acc_ref[inner + slots : inner + 2 * slots].astype(east_ref.dtype)


def edges_kernel(tile_cols, band_rows, slots, acc_ref, west_ref, east_ref, polar_ref, *out_refs):
    height = 5 * band_rows
    polar = polar_ref[0] != 0
    last = tile_cols - 1
    for r in range(height):
        out = out_refs[r // band_rows]
        row = (r % band_rows) * tile_cols
        second = (r + slots // 2) % slots
        from_west, from_east = west_ref[r].astype(jnp.float32), east_ref[r].astype(jnp.float32)
        for c in range(tile_cols):
            value = acc_ref[r * tile_cols + c]
            if c == 0:
                value = value + from_west
            if c == last:
                value = value + from_east
            if c == 1:
                value = value + jnp.where(polar, west_ref[second].astype(jnp.float32), 0.0)
            if c == last - 1:
                value = value + jnp.where(polar, east_ref[second].astype(jnp.float32), 0.0)
            out[row + c] = value.astype(out.dtype)


def pack_kernel(tile_cols, band_rows, slots, side_ref, *refs):
    bands, (west_ref, east_ref) = refs[:5], refs[5:]
    height, half = 5 * band_rows, slots // 2
    last = tile_cols - 1

    def block(r, c):
        return bands[r // band_rows][(r % band_rows) * tile_cols + c]

    for r in range(height):
        west_ref[r] = block(r, 0)
        east_ref[r] = block(r, last)
    for r in range(height, slots):
        west_ref[r] = block(0, 0)
        east_ref[r] = block(0, last)

    @pl.when(side_ref[0] == 1)
    def _():
        for r in range(height - half, height):
            west_ref[(r + half) % slots] = block(r, 1)
            east_ref[(r + half) % slots] = block(r, last - 1)

    @pl.when(side_ref[0] == 2)
    def _():
        for r in range(half):
            west_ref[(r + half) % slots] = block(r, 1)
            east_ref[(r + half) % slots] = block(r, last - 1)


def tangent_kernel(pos_ref, weights_ref, *refs):
    sources, out_ref, seen, sems = refs[:-3], refs[-3], refs[-2], refs[-1]
    targets, stencil, cells, _ = weights_ref.shape
    copies, at = [], 0
    for n, source in enumerate(sources):
        size = source.shape[0]
        copies.append(pltpu.make_async_copy(source, seen.at[pl.ds(at, size)], sems.at[n]))
        at += size
    for copy in copies:
        copy.start()
    for copy in copies:
        copy.wait()
    for t in range(targets):
        picked = [seen[pos_ref[t * stencil + k]] for k in range(stencil)]
        out_ref[t] = jnp.dot(
            jnp.concatenate(picked, axis=1),
            weights_ref[t].reshape(stencil * cells, cells),
            preferred_element_type=jnp.float32,
        ).astype(out_ref.dtype)


def on_device(perturbation, adjoint_forcing, source_rows, source_cols, cubic_weights):
    fields, levels, band_rows, tile_cols, cells = perturbation.shape
    stencil = source_rows.shape[2]
    rows = fields * levels
    targets = band_rows * tile_cols
    reach = 2 * band_rows
    height = band_rows + 2 * reach
    half = height - reach
    slots = 2 * half
    inner = height * tile_cols
    places = inner + 2 * slots
    bf16, f32 = jnp.bfloat16, jnp.float32

    band_index, tile_index = lax.axis_index("lat"), lax.axis_index("lon")
    first, final = band_index == 0, band_index == lax.axis_size("lat") - 1
    side = jnp.where(first, 1, jnp.where(final, 2, 0)).astype(jnp.int32).reshape(1)
    total_cols = tile_cols * lax.axis_size("lon")

    local_rows = source_rows - band_index * band_rows + reach
    local_cols = jnp.mod(source_cols - tile_index * tile_cols + 2, total_cols) - 2
    near = (local_cols == -1) | (local_cols == tile_cols)
    slot = jnp.where(near, local_rows, (local_rows + half) % slots)
    positions = jnp.where(
        (local_cols >= 0) & (local_cols < tile_cols),
        local_rows * tile_cols + local_cols,
        inner + slot + jnp.where(local_cols < 0, 0, slots),
    ).reshape(-1)

    def blocks_first(x):
        return jnp.transpose(x, (2, 3, 0, 1, 4)).reshape(targets, rows, cells)

    def blocks_last(x):
        return jnp.transpose(x.reshape(band_rows, tile_cols, fields, levels, cells), (2, 3, 0, 1, 4))

    weights = cubic_weights.reshape(targets, stencil, cells, cells)
    flops = 2 * rows * targets * stencil * cells * cells

    def shape(n, dtype=bf16):
        return jax.ShapeDtypeStruct((n, rows, cells), dtype)

    own = blocks_first(perturbation)
    lower_far = passed_along(own, "lat", 2)
    upper_far = passed_along(own, "lat", -2)

    forcing = blocks_first(adjoint_forcing)
    acc, west_part, east_part = pl.pallas_call(
        functools.partial(adjoint_kernel, tile_cols, height, slots),
        out_shape=(shape(places, f32), shape(slots), shape(slots)),
        in_specs=[SMEM, VMEM, VMEM],
        out_specs=(VMEM, VMEM, VMEM),
        compiler_params=PARAMS,
        cost_estimate=pl.CostEstimate(flops=flops, bytes_accessed=8 << 20, transcendentals=0),
        name="adjoint",
    )(positions, forcing, weights)
    from_east = shifted(west_part, "lon", -1)
    from_west = shifted(east_part, "lon", 1)

    lower_near = passed_along(own, "lat", 1)
    upper_near = passed_along(own, "lat", -1)

    to_lower_far, to_lower_near, kept, to_upper_near, to_upper_far = pl.pallas_call(
        functools.partial(edges_kernel, tile_cols, band_rows, slots),
        out_shape=(shape(targets), shape(targets), shape(targets, f32), shape(targets), shape(targets)),
        in_specs=[VMEM, VMEM, VMEM, SMEM],
        out_specs=(VMEM,) * 5,
        compiler_params=PARAMS,
        cost_estimate=pl.CostEstimate(flops=flops // 4, bytes_accessed=8 << 20, transcendentals=0),
        name="edges",
    )(acc, from_west, from_east, side)
    got = [
        passed_along(to_lower_far, "lat", -2),
        passed_along(to_upper_far, "lat", 2),
        passed_along(to_lower_near, "lat", -1),
        passed_along(to_upper_near, "lat", 1),
    ]

    bands = (lower_far, lower_near, own, upper_near, upper_far)
    west_strip, east_strip = pl.pallas_call(
        functools.partial(pack_kernel, tile_cols, band_rows, slots),
        out_shape=(shape(slots), shape(slots)),
        in_specs=[SMEM] + [VMEM] * 5,
        out_specs=(VMEM, VMEM),
        compiler_params=PARAMS,
        cost_estimate=pl.CostEstimate(flops=flops // 4, bytes_accessed=2 << 20, transcendentals=0),
        name="pack",
    )(side, *bands)
    east = shifted(west_strip, "lon", -1)
    west = shifted(east_strip, "lon", 1)
    tangent = pl.pallas_call(
        tangent_kernel,
        out_shape=shape(targets),
        in_specs=[SMEM, VMEM] + [ANY] * 7,
        out_specs=VMEM,
        scratch_shapes=[pltpu.VMEM((places, rows, cells), bf16), pltpu.SemaphoreType.DMA((7,))],
        compiler_params=PARAMS,
        cost_estimate=pl.CostEstimate(flops=flops, bytes_accessed=5 << 20, transcendentals=0),
        name="tangent",
    )(positions, weights, *bands, west, east)
    tangent_out = blocks_last(tangent)

    adjoint = kept
    for part in got:
        adjoint = adjoint + part.astype(f32)
    return (tangent_out, blocks_last(adjoint.astype(bf16)))


def solution(mesh):
    placed = (
        P("member", "lev", "lat", "lon", None),
        P("member", "lev", "lat", "lon", None),
        P("lat", "lon", None),
        P("lat", "lon", None),
        P("lat", "lon", None, None, None),
    )
    return jax.shard_map(
        on_device,
        mesh=mesh,
        in_specs=placed,
        out_specs=(P("member", "lev", "lat", "lon", None), P("member", "lev", "lat", "lon", None)),
        check_vma=False,
    )
```

time: 134 us -> 95.8 us (0.71)
  the two profiles are of different devices: /device:TPU:288 before, /device:TPU:36 now
where the time goes in v1:
time: 95.8 us; the launch traced here: 95.2 us
  starting transfers between devices  40.7 us (42%)
  waiting for transfers between devices  39.6 us (41%)
  local copies, waits for them, and re-layouts  9.68 us (10%)
  Pallas kernels  3.48 us (4%)
    ppermute x4, waiting for transfers between devices, shifted(): lax.ppermute(array, axis, [(i, (i + by) % devices) for i in range(devices)])  39.5 us
    ppermute x8, starting transfers between devices, passed_along(): return lax.ppermute(array, axis, pairs)  27.1 us
    ppermute x4, starting transfers between devices, shifted(): lax.ppermute(array, axis, [(i, (i + by) % devices) for i in range(devices)])  13.5 us
    unnamed x8, local copies, waits for them, and re-layouts  5.73 us
    transpose x2, local copies, waits for them, and re-layouts, blocks_first(): return jnp.transpose(x, (2, 3, 0, 1, 4)).reshape(targets, rows, cells)  2.04 us
  transfers between devices with their start and end apart: 12, of which 3 were waited for; matrix products, arithmetic and copies ran while one was open for 2% of the time, Pallas kernels for 0%

profile of v1, /device:TPU:36, one launch (start us, length us, event | category | flops | bytes accessed | tf_op | source)
XLA Modules:
  0.0 95.2 jit_solution(2703925122288315601)
XLA Ops:
  1.5 1.0 %copy.9 = bf16[4,4,2,32,128]{4,3,2,1,0:T(8,128)(2,1)S(1)} copy(bf16[4,4,2,32,128]{4,1,0,3,2:T(4,128)(2,1)} %bitcast.25) | data formatting | bytes 524288 | tf_op jit(solution)/shard_map/transpose | solution.py:145
  2.5 1.6 %copy-done = bf16[4,4,4,128,128]{4,3,2,1,0:T(8,128)(2,1)S(1)} copy-done((bf16[4,4,4,128,128]{4,3,2,1,0:T(8,128)(2,1)S(1)}, bf16[4,4,4,128,128]{4,3,2,1,0:T(8,128)(2,1)}, u32[]{:S(2)}) %copy-start) | copy-done | bytes 2097176
  4.1 1.5 %adjoint.1 = (f32[128,64,128]{2,1,0:T(8,128)S(1)}, bf16[24,64,128]{2,1,0:T(8,128)(2,1)S(1)}, bf16[24,64,128]{2,1,0:T(8,128)(2,1)S(1)}) custom-call(s32[64]{0:T(128)S(1)} %reshape.25.pos_ref, bf16[16,64,128]{2,1,0:T(8,128)(2,1)S(1)} %bitcast.23, bf16[16,4,128,128]{3,2,1,0:T(8,128)(2,1)S(1)} %bitcast.14), custom_call_target="tpu_custom_call" | custom-call | flops 134217728 | bytes 8388608 | tf_op jit(solution)/shard_map/adjoint/pallas_call | solution.py:161
  5.6 1.9 %copy-done.2 = f32[128,64,128]{2,1,0:T(8,128)} copy-done((f32[128,64,128]{2,1,0:T(8,128)}, f32[128,64,128]{2,1,0:T(8,128)S(1)}, u32[]{:S(2)}) %copy-start.2) | copy-done | bytes 4194328
  7.6 3.3 %collective-permute-start.6 = (bf16[24,64,128]{2,1,0:T(8,128)(2,1)S(1)}, bf16[24,64,128]{2,1,0:T(8,128)(2,1)S(1)}, u32[]{:S(2)}, u32[]{:S(2)}) collective-permute-start(bf16[24,64,128]{2,1,0:T(8,128)(2,1)S(1)} %get-tuple-element.15), channel_id=1, source_target_pairs={{0,2},{2,4},{4,6},{6,0},{1,3},{3,5},{5,7},{7,1},{8,10},{10,12},{12... | collective-permute-start | bytes 1179656 | tf_op jit(solution)/shard_map/ppermute | solution.py:24
  10.8 2.6 %collective-permute-start.7 = (bf16[24,64,128]{2,1,0:T(8,128)(2,1)S(1)}, bf16[24,64,128]{2,1,0:T(8,128)(2,1)S(1)}, u32[]{:S(2)}, u32[]{:S(2)}) collective-permute-start(bf16[24,64,128]{2,1,0:T(8,128)(2,1)S(1)} %get-tuple-element.16), channel_id=1, source_target_pairs={{0,6},{2,0},{4,2},{6,4},{1,7},{3,1},{5,3},{7,5},{8,14},{10,8},{12,... | collective-permute-start | bytes 1179656 | tf_op jit(solution)/shard_map/ppermute | solution.py:24
  13.5 1.0 %copy.7 = bf16[4,4,2,32,128]{4,3,2,1,0:T(8,128)(2,1)S(1)} copy(bf16[4,4,2,32,128]{4,1,0,3,2:T(4,128)(2,1)} %bitcast.26) | data formatting | bytes 524288 | tf_op jit(solution)/shard_map/transpose | solution.py:145
  14.5 6.9 %collective-permute-start = (bf16[16,64,128]{2,1,0:T(8,128)(2,1)S(1)}, bf16[16,64,128]{2,1,0:T(8,128)(2,1)S(1)}, u32[]{:S(2)}, u32[]{:S(2)}) collective-permute-start(bf16[16,64,128]{2,1,0:T(8,128)(2,1)S(1)} %bitcast.16), channel_id=1, source_target_pairs={{0,16},{8,24},{16,32},{24,40},{32,48},{40,56},{48,64},{56,72},{64,... | collective-permute-start | bytes 786440 | tf_op jit(solution)/shard_map/ppermute | solution.py:19
  21.4 4.7 %collective-permute-start.1 = (bf16[16,64,128]{2,1,0:T(8,128)(2,1)S(1)}, bf16[16,64,128]{2,1,0:T(8,128)(2,1)S(1)}, u32[]{:S(2)}, u32[]{:S(2)}) collective-permute-start(bf16[16,64,128]{2,1,0:T(8,128)(2,1)S(1)} %bitcast.17), channel_id=1, source_target_pairs={{0,8},{8,16},{16,24},{24,32},{32,40},{40,48},{48,56},{56,64},{64,7... | collective-permute-start | bytes 786440 | tf_op jit(solution)/shard_map/ppermute | solution.py:19
  26.2 1.3 %collective-permute-start.2 = (bf16[16,64,128]{2,1,0:T(8,128)(2,1)S(1)}, bf16[16,64,128]{2,1,0:T(8,128)(2,1)S(1)}, u32[]{:S(2)}, u32[]{:S(2)}) collective-permute-start(bf16[16,64,128]{2,1,0:T(8,128)(2,1)S(1)} %bitcast.18), channel_id=1, source_target_pairs={{8,0},{16,8},{24,16},{32,24},{40,32},{48,40},{56,48},{64,56},{72,6... | collective-permute-start | bytes 786440 | tf_op jit(solution)/shard_map/ppermute | solution.py:19
  27.5 1.3 %collective-permute-start.3 = (bf16[16,64,128]{2,1,0:T(8,128)(2,1)S(1)}, bf16[16,64,128]{2,1,0:T(8,128)(2,1)S(1)}, u32[]{:S(2)}, u32[]{:S(2)}) collective-permute-start(bf16[16,64,128]{2,1,0:T(8,128)(2,1)S(1)} %bitcast.19), channel_id=1, source_target_pairs={{16,0},{24,8},{32,16},{40,24},{48,32},{56,40},{64,48},{72,56},{80,... | collective-permute-start | bytes 786440 | tf_op jit(solution)/shard_map/ppermute | solution.py:19
  28.8 32.9 %collective-permute-done.7.east_ref = bf16[24,64,128]{2,1,0:T(8,128)(2,1)S(1)} collective-permute-done((bf16[24,64,128]{2,1,0:T(8,128)(2,1)S(1)}, bf16[24,64,128]{2,1,0:T(8,128)(2,1)S(1)}, u32[]{:S(2)}, u32[]{:S(2)}) %collective-permute-start.7) | collective-permute-done | bytes 393248 | tf_op jit(solution)/shard_map/ppermute | solution.py:24
  61.8 2.2 %copy-done.3 = f32[128,64,128]{2,1,0:T(8,128)S(1)} copy-done((f32[128,64,128]{2,1,0:T(8,128)S(1)}, f32[128,64,128]{2,1,0:T(8,128)}, u32[]{:S(2)}) %copy-start.3) | copy-done | bytes 4194328
  64.3 1.4 %collective-permute-start.10 = (bf16[16,64,128]{2,1,0:T(8,128)(2,1)S(1)}, bf16[16,64,128]{2,1,0:T(8,128)(2,1)S(1)}, u32[]{:S(2)}, u32[]{:S(2)}) collective-permute-start(bf16[16,64,128]{2,1,0:T(8,128)(2,1)S(1)} %get-tuple-element.20), channel_id=1, source_target_pairs={{8,0},{16,8},{24,16},{32,24},{40,32},{48,40},{56,48},{64,56},{72,6... | collective-permute-start | bytes 786440 | tf_op jit(solution)/shard_map/ppermute | solution.py:19
  65.7 4.6 %collective-permute-start.11 = (bf16[16,64,128]{2,1,0:T(8,128)(2,1)S(1)}, bf16[16,64,128]{2,1,0:T(8,128)(2,1)S(1)}, u32[]{:S(2)}, u32[]{:S(2)}) collective-permute-start(bf16[16,64,128]{2,1,0:T(8,128)(2,1)S(1)} %get-tuple-element.21), channel_id=1, source_target_pairs={{0,8},{8,16},{16,24},{24,32},{32,40},{40,48},{48,56},{56,64},{64,7... | collective-permute-start | bytes 786440 | tf_op jit(solution)/shard_map/ppermute | solution.py:19
  70.3 1.3 %collective-permute-start.8 = (bf16[16,64,128]{2,1,0:T(8,128)(2,1)S(1)}, bf16[16,64,128]{2,1,0:T(8,128)(2,1)S(1)}, u32[]{:S(2)}, u32[]{:S(2)}) collective-permute-start(bf16[16,64,128]{2,1,0:T(8,128)(2,1)S(1)} %get-tuple-element.18), channel_id=1, source_target_pairs={{16,0},{24,8},{32,16},{40,24},{48,32},{56,40},{64,48},{72,56},{80,... | collective-permute-start | bytes 786440 | tf_op jit(solution)/shard_map/ppermute | solution.py:19
  71.7 5.5 %collective-permute-start.9 = (bf16[16,64,128]{2,1,0:T(8,128)(2,1)S(1)}, bf16[16,64,128]{2,1,0:T(8,128)(2,1)S(1)}, u32[]{:S(2)}, u32[]{:S(2)}) collective-permute-start(bf16[16,64,128]{2,1,0:T(8,128)(2,1)S(1)} %get-tuple-element.19), channel_id=1, source_target_pairs={{0,16},{8,24},{16,32},{24,40},{32,48},{40,56},{48,64},{56,72},{64,... | collective-permute-start | bytes 786440 | tf_op jit(solution)/shard_map/ppermute | solution.py:19
  77.3 5.7 %collective-permute-start.4 = (bf16[24,64,128]{2,1,0:T(8,128)(2,1)S(1)}, bf16[24,64,128]{2,1,0:T(8,128)(2,1)S(1)}, u32[]{:S(2)}, u32[]{:S(2)}) collective-permute-start(bf16[24,64,128]{2,1,0:T(8,128)(2,1)S(1)} %get-tuple-element.12), channel_id=1, source_target_pairs={{0,2},{2,4},{4,6},{6,0},{1,3},{3,5},{5,7},{7,1},{8,10},{10,12},{12... | collective-permute-start | bytes 1179656 | tf_op jit(solution)/shard_map/ppermute | solution.py:24
  83.0 2.0 %collective-permute-start.5 = (bf16[24,64,128]{2,1,0:T(8,128)(2,1)S(1)}, bf16[24,64,128]{2,1,0:T(8,128)(2,1)S(1)}, u32[]{:S(2)}, u32[]{:S(2)}) collective-permute-start(bf16[24,64,128]{2,1,0:T(8,128)(2,1)S(1)} %get-tuple-element.13), channel_id=1, source_target_pairs={{0,6},{2,0},{4,2},{6,4},{1,7},{3,1},{5,3},{7,5},{8,14},{10,8},{12,... | collective-permute-start | bytes 1179656 | tf_op jit(solution)/shard_map/ppermute | solution.py:24
  85.2 0.9 copy.13
  86.1 2.2 %collective-permute-done.4.refs_5_ = bf16[24,64,128]{2,1,0:T(8,128)(2,1)S(1)} collective-permute-done((bf16[24,64,128]{2,1,0:T(8,128)(2,1)S(1)}, bf16[24,64,128]{2,1,0:T(8,128)(2,1)S(1)}, u32[]{:S(2)}, u32[]{:S(2)}) %collective-permute-start.4) | collective-permute-done | bytes 393248 | tf_op jit(solution)/shard_map/ppermute | solution.py:24
  88.2 4.4 %collective-permute-done.5.refs_6_ = bf16[24,64,128]{2,1,0:T(8,128)(2,1)S(1)} collective-permute-done((bf16[24,64,128]{2,1,0:T(8,128)(2,1)S(1)}, bf16[24,64,128]{2,1,0:T(8,128)(2,1)S(1)}, u32[]{:S(2)}, u32[]{:S(2)}) %collective-permute-start.5) | collective-permute-done | bytes 393248 | tf_op jit(solution)/shard_map/ppermute | solution.py:24
  92.7 1.6 %tangent.1 = bf16[16,64,128]{2,1,0:T(8,128)(2,1)S(1)} custom-call(s32[64]{0:T(128)S(1)} %reshape.25.pos_ref, bf16[16,4,128,128]{3,2,1,0:T(8,128)(2,1)S(1)} %bitcast.15, bf16[16,64,128]{2,1,0:T(8,128)(2,1)S(1)} %collective-permute-done.refs_0_, bf16[16,64,128]{2,1,0:T(8,128)(2,1)S(1)} %collective-permute-done.1.refs_1_, bf16[16,64,128]{2,1,0:T(8,128)(2,1)S(1)} %bitcast.21, ...), custom_call_target="tpu_custom_call" | custom-call | flops 134217728 | bytes 5242880 | tf_op jit(solution)/shard_map/tangent/pallas_call | solution.py:204
  94.3 0.9 copy.14
  (19 shorter events, 1.5 us)
Async XLA Ops:
  2.5 1.6 %copy-start = (bf16[4,4,4,128,128]{4,3,2,1,0:T(8,128)(2,1)S(1)}, bf16[4,4,4,128,128]{4,3,2,1,0:T(8,128)(2,1)}, u32[]{:S(2)}) copy-start(bf16[4,4,4,128,128]{4,3,2,1,0:T(8,128)(2,1)} %param.9) | copy-start | bytes 6291460
  5.6 2.0 %copy-start.2 = (f32[128,64,128]{2,1,0:T(8,128)}, f32[128,64,128]{2,1,0:T(8,128)S(1)}, u32[]{:S(2)}) copy-start(f32[128,64,128]{2,1,0:T(8,128)S(1)} %get-tuple-element.14.acc_ref) | copy-start | bytes 12582916
  7.6 19.9 %collective-permute-start.6 = (bf16[24,64,128]{2,1,0:T(8,128)(2,1)S(1)}, bf16[24,64,128]{2,1,0:T(8,128)(2,1)S(1)}, u32[]{:S(2)}, u32[]{:S(2)}) collective-permute-start(bf16[24,64,128]{2,1,0:T(8,128)(2,1)S(1)} %get-tuple-element.15), channel_id=1, source_target_pairs={{0,2},{2,4},{4,6},{6,0},{1,3},{3,5},{5,7},{7,1},{8,10},{10,12},{12... | collective-permute-start | bytes 1179656 | tf_op jit(solution)/shard_map/ppermute | solution.py:24
  10.8 50.9 %collective-permute-start.7 = (bf16[24,64,128]{2,1,0:T(8,128)(2,1)S(1)}, bf16[24,64,128]{2,1,0:T(8,128)(2,1)S(1)}, u32[]{:S(2)}, u32[]{:S(2)}) collective-permute-start(bf16[24,64,128]{2,1,0:T(8,128)(2,1)S(1)} %get-tuple-element.16), channel_id=1, source_target_pairs={{0,6},{2,0},{4,2},{6,4},{1,7},{3,1},{5,3},{7,5},{8,14},{10,8},{12,... | collective-permute-start | bytes 1179656 | tf_op jit(solution)/shard_map/ppermute | solution.py:24
  14.5 51.2 %collective-permute-start = (bf16[16,64,128]{2,1,0:T(8,128)(2,1)S(1)}, bf16[16,64,128]{2,1,0:T(8,128)(2,1)S(1)}, u32[]{:S(2)}, u32[]{:S(2)}) collective-permute-start(bf16[16,64,128]{2,1,0:T(8,128)(2,1)S(1)} %bitcast.16), channel_id=1, source_target_pairs={{0,16},{8,24},{16,32},{24,40},{32,48},{40,56},{48,64},{56,72},{64,... | collective-permute-start | bytes 786440 | tf_op jit(solution)/shard_map/ppermute | solution.py:19
  21.4 48.9 %collective-permute-start.1 = (bf16[16,64,128]{2,1,0:T(8,128)(2,1)S(1)}, bf16[16,64,128]{2,1,0:T(8,128)(2,1)S(1)}, u32[]{:S(2)}, u32[]{:S(2)}) collective-permute-start(bf16[16,64,128]{2,1,0:T(8,128)(2,1)S(1)} %bitcast.17), channel_id=1, source_target_pairs={{0,8},{8,16},{16,24},{24,32},{32,40},{40,48},{48,56},{56,64},{64,7... | collective-permute-start | bytes 786440 | tf_op jit(solution)/shard_map/ppermute | solution.py:19
  26.2 45.5 %collective-permute-start.2 = (bf16[16,64,128]{2,1,0:T(8,128)(2,1)S(1)}, bf16[16,64,128]{2,1,0:T(8,128)(2,1)S(1)}, u32[]{:S(2)}, u32[]{:S(2)}) collective-permute-start(bf16[16,64,128]{2,1,0:T(8,128)(2,1)S(1)} %bitcast.18), channel_id=1, source_target_pairs={{8,0},{16,8},{24,16},{32,24},{40,32},{48,40},{56,48},{64,56},{72,6... | collective-permute-start | bytes 786440 | tf_op jit(solution)/shard_map/ppermute | solution.py:19
  27.5 49.7 %collective-permute-start.3 = (bf16[16,64,128]{2,1,0:T(8,128)(2,1)S(1)}, bf16[16,64,128]{2,1,0:T(8,128)(2,1)S(1)}, u32[]{:S(2)}, u32[]{:S(2)}) collective-permute-start(bf16[16,64,128]{2,1,0:T(8,128)(2,1)S(1)} %bitcast.19), channel_id=1, source_target_pairs={{16,0},{24,8},{32,16},{40,24},{48,32},{56,40},{64,48},{72,56},{80,... | collective-permute-start | bytes 786440 | tf_op jit(solution)/shard_map/ppermute | solution.py:19
  61.8 2.2 %copy-start.3 = (f32[128,64,128]{2,1,0:T(8,128)S(1)}, f32[128,64,128]{2,1,0:T(8,128)}, u32[]{:S(2)}) copy-start(f32[128,64,128]{2,1,0:T(8,128)} %copy-done.2) | copy-start | bytes 12582916
  63.9 28.7 %copy-start.1 = (bf16[4,4,4,128,128]{4,3,2,1,0:T(8,128)(2,1)S(1)}, bf16[4,4,4,128,128]{4,3,2,1,0:T(8,128)(2,1)}, u32[]{:S(2)}) copy-start(bf16[4,4,4,128,128]{4,3,2,1,0:T(8,128)(2,1)} %param.9) | copy-start | bytes 6291460
  64.3 18.7 %collective-permute-start.10 = (bf16[16,64,128]{2,1,0:T(8,128)(2,1)S(1)}, bf16[16,64,128]{2,1,0:T(8,128)(2,1)S(1)}, u32[]{:S(2)}, u32[]{:S(2)}) collective-permute-start(bf16[16,64,128]{2,1,0:T(8,128)(2,1)S(1)} %get-tuple-element.20), channel_id=1, source_target_pairs={{8,0},{16,8},{24,16},{32,24},{40,32},{48,40},{56,48},{64,56},{72,6... | collective-permute-start | bytes 786440 | tf_op jit(solution)/shard_map/ppermute | solution.py:19
  65.7 19.2 %collective-permute-start.11 = (bf16[16,64,128]{2,1,0:T(8,128)(2,1)S(1)}, bf16[16,64,128]{2,1,0:T(8,128)(2,1)S(1)}, u32[]{:S(2)}, u32[]{:S(2)}) collective-permute-start(bf16[16,64,128]{2,1,0:T(8,128)(2,1)S(1)} %get-tuple-element.21), channel_id=1, source_target_pairs={{0,8},{8,16},{16,24},{24,32},{32,40},{40,48},{48,56},{56,64},{64,7... | collective-permute-start | bytes 786440 | tf_op jit(solution)/shard_map/ppermute | solution.py:19
  70.3 14.6 %collective-permute-start.8 = (bf16[16,64,128]{2,1,0:T(8,128)(2,1)S(1)}, bf16[16,64,128]{2,1,0:T(8,128)(2,1)S(1)}, u32[]{:S(2)}, u32[]{:S(2)}) collective-permute-start(bf16[16,64,128]{2,1,0:T(8,128)(2,1)S(1)} %get-tuple-element.18), channel_id=1, source_target_pairs={{16,0},{24,8},{32,16},{40,24},{48,32},{56,40},{64,48},{72,56},{80,... | collective-permute-start | bytes 786440 | tf_op jit(solution)/shard_map/ppermute | solution.py:19
  71.7 13.3 %collective-permute-start.9 = (bf16[16,64,128]{2,1,0:T(8,128)(2,1)S(1)}, bf16[16,64,128]{2,1,0:T(8,128)(2,1)S(1)}, u32[]{:S(2)}, u32[]{:S(2)}) collective-permute-start(bf16[16,64,128]{2,1,0:T(8,128)(2,1)S(1)} %get-tuple-element.19), channel_id=1, source_target_pairs={{0,16},{8,24},{16,32},{24,40},{32,48},{40,56},{48,64},{56,72},{64,... | collective-permute-start | bytes 786440 | tf_op jit(solution)/shard_map/ppermute | solution.py:19
  77.3 11.0 %collective-permute-start.4 = (bf16[24,64,128]{2,1,0:T(8,128)(2,1)S(1)}, bf16[24,64,128]{2,1,0:T(8,128)(2,1)S(1)}, u32[]{:S(2)}, u32[]{:S(2)}) collective-permute-start(bf16[24,64,128]{2,1,0:T(8,128)(2,1)S(1)} %get-tuple-element.12), channel_id=1, source_target_pairs={{0,2},{2,4},{4,6},{6,0},{1,3},{3,5},{5,7},{7,1},{8,10},{10,12},{12... | collective-permute-start | bytes 1179656 | tf_op jit(solution)/shard_map/ppermute | solution.py:24
  83.0 9.7 %collective-permute-start.5 = (bf16[24,64,128]{2,1,0:T(8,128)(2,1)S(1)}, bf16[24,64,128]{2,1,0:T(8,128)(2,1)S(1)}, u32[]{:S(2)}, u32[]{:S(2)}) collective-permute-start(bf16[24,64,128]{2,1,0:T(8,128)(2,1)S(1)} %get-tuple-element.13), channel_id=1, source_target_pairs={{0,6},{2,0},{4,2},{6,4},{1,7},{3,1},{5,3},{7,5},{8,14},{10,8},{12,... | collective-permute-start | bytes 1179656 | tf_op jit(solution)/shard_map/ppermute | solution.py:24
